TPU v7x, 32 devices: a whole 2x2x4 slice. The times are simulated.
32 devices in a mesh: group: 2 (over y), row: 4 (over z), col: 4 (over x, core).
Axes of the slice: x: 2, y: 2, z: 4, core: 2. Of those that a mesh axis runs over, the one named last changes fastest.
Arguments:
- compressed_absorbed_queries: bfloat16 [16, 128, 512], P(('group', 'row')), parts along dimension 0, may hold values from -6 to 6
- query_rope: bfloat16 [16, 64, 128], P(('group', 'row')), parts along dimension 0, may hold values from -6 to 6
- compressed_stored_keys: bfloat16 [16, 1024, 512], P(('group', 'row'), 'col'), parts along dimension 0, may hold values from -32 to 32
- cache_rope: bfloat16 [16, 64, 1024], P(('group', 'row'), None, 'col'), parts along dimension 0, may hold values from -32 to 32
- seq_lengths: int32 [16], P(('group', 'row')), parts along dimension 0, may hold values from 2 to 1024, as said below
- ffn_rows: bfloat16 [64, 7168], P(('group', 'row'), 'col'), parts along dimension 0, may hold values from -6 to 6
- norm_gain: bfloat16 [7168], P('col'), may hold values from 0.099609375 to 1.8984375
- w_gate: bfloat16 [7168, 18432], P('col', 'row'), may hold values from -0.0625 to 0.0625
- w_up: bfloat16 [7168, 18432], P('col', 'row'), may hold values from -0.0625 to 0.0625
- w_down: bfloat16 [18432, 7168], P('row', 'col'), may hold values from -0.046875 to 0.046875
Outputs:
- context: bfloat16 [16, 128, 512], P(('group', 'row'), 'col'), parts along dimension 0
- ffn_out: bfloat16 [64, 7168], P(('group', 'row'), 'col'), parts along dimension 0
There are 2 independent parts, one for each index of `group`. A program takes and returns all parts, laid end to end along the dimension named above; an argument that names none is the same for every part. Nothing has to cross between parts.
Inputs may be any that keep to these rules, and one draw needn't show every extreme that they name: `seq_lengths`: each sequence has 2 to 1024 filled slots, the first ones of its cache, and some sequence has exactly 1024.
All inputs are finite; a program needn't handle non-finite values.
Results may differ from a plain program's by a relative error of at most 0.017.
Values may be sent and summed in bfloat16 or wider, within the bound.
A program may use at most 128 MiB of HBM per device.

v0:
```python
import jax
import jax.numpy as jnp
from jax import lax
from jax.sharding import PartitionSpec as P

NOPE = 128
NEGATIVE_PADDING = -1e30


def joined(x, axis, combine):
    everything = jax.tree.map(
        lambda part, kind: lax.all_gather(part.astype(kind), axis),
        x,
        (jnp.bfloat16, jnp.bfloat16, jnp.bfloat16),
    )

    def take(k):
        return jax.tree.map(lambda part, own: part[k].astype(own.dtype), everything, x)

    return lax.fori_loop(
        1, lax.axis_size(axis), lambda k, so_far: combine(so_far, take(k)), take(0)
    )


def local_partials(
    compressed_absorbed_queries,
    query_rope,
    compressed_stored_keys,
    cache_rope,
    seq_lengths,
    first_pos,
):
    similarity_logits = jnp.einsum(
        "zxm,zum->zxu",
        compressed_absorbed_queries,
        compressed_stored_keys,
        preferred_element_type=jnp.float32,
    )
    similarity_logits = similarity_logits + jnp.einsum(
        "srh,srl->shl", query_rope, cache_rope, preferred_element_type=jnp.float32
    )
    similarity_logits = similarity_logits * (NOPE + query_rope.shape[1]) ** (-0.5)
    position = first_pos + jnp.arange(compressed_stored_keys.shape[1], dtype=jnp.int32)
    visible = position[None, None, :] < seq_lengths[:, None, None]
    similarity_logits = jnp.where(visible, similarity_logits, NEGATIVE_PADDING)
    top_score = jnp.max(similarity_logits, axis=2)
    weights = jnp.where(visible, jnp.exp(similarity_logits - top_score[:, :, None]), 0.0)
    denominator = jnp.sum(weights, axis=2)
    weighted = jnp.einsum(
        "jac,jcw->jaw",
        weights.astype(jnp.bfloat16),
        compressed_stored_keys,
        preferred_element_type=jnp.float32,
    )
    return (top_score, denominator, weighted)


def join_partials(earlier, later):
    top_score = jnp.maximum(earlier[0], later[0])
    left_factor = jnp.exp(earlier[0] - top_score)
    right_factor = jnp.exp(later[0] - top_score)
    denominator = earlier[1] * left_factor + later[1] * right_factor
    weighted = earlier[2] * left_factor[:, :, None] + later[2] * right_factor[:, :, None]
    return (top_score, denominator, weighted)


def on_device(
    compressed_absorbed_queries,
    query_rope,
    compressed_stored_keys,
    cache_rope,
    seq_lengths,
    ffn_rows,
    norm_gain,
    w_gate,
    w_up,
    w_down,
):
    column_position = lax.axis_index("col")
    first_pos = column_position * compressed_stored_keys.shape[1]
    top_score, denominator, weighted = local_partials(
        compressed_absorbed_queries,
        query_rope,
        compressed_stored_keys,
        cache_rope,
        seq_lengths,
        first_pos,
    )
    head_share = compressed_absorbed_queries.shape[1] // lax.axis_size("col")
    merged = joined((top_score, denominator, weighted), "col", join_partials)
    own_total = lax.dynamic_slice_in_dim(merged[1], column_position * head_share, head_share, 1)
    own_weighted = lax.dynamic_slice_in_dim(merged[2], column_position * head_share, head_share, 1)
    context = (own_weighted / own_total[:, :, None]).astype(jnp.bfloat16)
    rows_wide = ffn_rows.astype(jnp.float32)
    square_sums = lax.psum(jnp.sum(rows_wide * rows_wide, axis=1), "col")
    full_width = ffn_rows.shape[1] * lax.axis_size("col")
    reciprocal_norm = lax.rsqrt(square_sums / full_width + 1e-06)
    normed = (rows_wide * reciprocal_norm[:, None] * norm_gain.astype(jnp.float32)[None, :]).astype(
        jnp.bfloat16
    )
    shard_rows = lax.all_gather(normed, "row", axis=0, tiled=True)
    gate_part = jnp.dot(shard_rows, w_gate, preferred_element_type=jnp.float32)
    up_part = jnp.dot(shard_rows, w_up, preferred_element_type=jnp.float32)
    projected = jnp.concatenate([gate_part, up_part], axis=1)
    units = w_gate.shape[1]
    share_sums = lax.psum_scatter(
        projected.astype(jnp.bfloat16), "col", scatter_dimension=0, tiled=True
    ).astype(jnp.float32)
    hidden_share = (jax.nn.silu(share_sums[:, :units]) * share_sums[:, units:]).astype(jnp.bfloat16)
    hidden = lax.all_gather(hidden_share, "col", axis=0, tiled=True)
    reduced_total = lax.psum_scatter(
        jnp.dot(hidden, w_down, preferred_element_type=jnp.float32),
        "row",
        scatter_dimension=0,
        tiled=True,
    )
    ffn_out = (rows_wide + reduced_total).astype(jnp.bfloat16)
    return (context, ffn_out)


def solution(mesh):
    return jax.shard_map(
        on_device,
        mesh=mesh,
        in_specs=(
            P(("group", "row"), None, None),
            P(("group", "row"), None, None),
            P(("group", "row"), "col", None),
            P(("group", "row"), None, "col"),
            P(("group", "row")),
            P(("group", "row"), "col"),
            P("col"),
            P("col", "row"),
            P("col", "row"),
            P("row", "col"),
        ),
        out_specs=(P(("group", "row"), "col", None), P(("group", "row"), "col")),
        check_vma=False,
    )
```

profile of v0, /device:TPU:0, one launch (start us, length us, event | category | flops | bytes accessed | tf_op | source)
XLA Modules:
  0.0 115.1 jit_solution(4013423057301016343)
XLA Ops:
  7.2 0.0 copy-start
  7.2 0.0 reduce-scatter.3.cloned.1.call-start
  7.2 0.9 fusion.14
  8.2 0.7 convert_element_type.125
  8.8 8.3 %psum.7 = f32[8]{0:T(128)S(1)} all-reduce(f32[8]{0:T(128)S(1)} %fusion.14), channel_id=1, replica_groups=mesh['group'=2,'row'=4,'col'=4] {'col'}, use_global_device_ids=true, to_apply=%region_5.6 | all-reduce | flops 8 | bytes 64 | tf_op jit(solution)/shard_map/psum | solution.py:95
  17.2 1.0 fusion.16
  18.2 13.7 %all_gather.24 = bf16[32,1792]{1,0:T(8,128)(2,1)S(1)} all-gather(bf16[8,1792]{1,0:T(8,128)(2,1)S(1)} %fusion.16), channel_id=1, replica_groups=mesh['group'=2,'row'=4,'col'=4] {'row'}, dimensions={0}, use_global_device_ids=true | all-gather | bytes 143360 | tf_op jit(solution)/shard_map/all_gather | solution.py:101
  31.9 8.6 %convolution_convert_fusion = bf16[32,4608]{1,0:T(8,128)(2,1)S(1)} fusion(bf16[32,1792]{1,0:T(8,128)(2,1)S(1)} %all_gather.24, bf16[1792,4608]{1,0:T(8,128)(2,1)} %param.20), kind=kOutput, calls=%fused_computation.12 | convolution fusion | flops 528629760 | bytes 16924672 | tf_op jit(solution)/shard_map/dot_general | solution.py:103
  40.5 0.0 copy-done.1
  40.5 0.0 copy-start.4
  40.5 0.0 copy-start.5
  40.6 0.0 copy-start.2
  40.6 2.9 %convolution_convert_fusion.1 = bf16[32,4608]{1,0:T(8,128)(2,1)S(1)} fusion(bf16[32,1792]{1,0:T(8,128)(2,1)S(1)} %all_gather.24, bf16[1792,4608]{1,0:T(8,128)(2,1)S(1)} %copy-done.1), kind=kOutput, calls=%fused_computation.13 | convolution fusion | flops 528629760 | bytes 16924672 | tf_op jit(solution)/shard_map/dot_general | solution.py:102
  43.5 0.9 pad_maximum_fusion
  44.4 0.0 reduce-scatter.3.cloned.1.call-update
  44.4 0.0 all-gather.7.cloned.1.call-start
  44.4 0.0 copy-done.6
  44.5 0.1 broadcast_compare_fusion
  44.5 0.0 copy-done.4
  44.5 0.0 copy-done.5
  44.5 0.2 fusion.23
  44.8 0.0 copy-done
  44.8 0.0 copy-done.2
  44.8 0.4 fusion.22
  45.2 1.0 convolution_convert_fusion.2
  46.2 0.0 all-gather.7.cloned.1.call-update
  46.2 0.0 reduce-scatter.5.cloned.1.call-start
  46.2 0.2 fusion.8
  46.4 5.1 %all-gather.4 = bf16[4,2,128]{2,1,0:T(2,128)(2,1)S(1)} all-gather(bf16[1,2,128]{2,1,0:T(2,128)(2,1)S(1)} %bitcast.49), channel_id=3, replica_groups=mesh['group'=2,'row'=4,'col'=4] {'col'}, dimensions={0}, use_global_device_ids=true | all-gather | bytes 2560 | tf_op jit(solution)/shard_map/all_gather | solution.py:12
  51.5 5.0 %all-gather.3 = bf16[4,2,128]{2,1,0:T(2,128)(2,1)S(1)} all-gather(bf16[1,2,128]{2,1,0:T(2,128)(2,1)S(1)} %convert_bitcast_fusion.1), channel_id=2, replica_groups=mesh['group'=2,'row'=4,'col'=4] {'col'}, dimensions={0}, use_global_device_ids=true | all-gather | bytes 2560 | tf_op jit(solution)/shard_map/all_gather | solution.py:12
  56.6 10.2 %reduce-scatter.3.cloned.1.call-done = bf16[8,9216]{1,0:T(8,128)(2,1)} async-done(((bf16[32,9216]{1,0:T(8,128)(2,1)}), bf16[8,9216]{1,0:T(8,128)(2,1)}) %reduce-scatter.3.cloned.1.call-update) | async-done | bytes 147472 | tf_op jit(solution)/shard_map/reduce_scatter | solution.py:106
  66.8 0.9 convert_element_type.127
  67.7 0.1 fusion.9
  67.8 0.0 copy-start.3
  67.8 5.9 %all_gather.25 = bf16[32,4608]{1,0:T(8,128)(2,1)S(1)} all-gather(bf16[8,4608]{1,0:T(8,128)(2,1)S(1)} %fusion.9), channel_id=1, replica_groups=mesh['group'=2,'row'=4,'col'=4] {'col'}, dimensions={0}, use_global_device_ids=true | all-gather | bytes 368640 | tf_op jit(solution)/shard_map/all_gather | solution.py:110
  73.6 9.6 %fusion.24 = f32[32,1792]{1,0:T(8,128)} fusion(bf16[32,4608]{1,0:T(8,128)(2,1)S(1)} %all_gather.25, bf16[4608,1792]{1,0:T(8,128)(2,1)} %param.21), kind=kOutput, calls=%fused_computation.49 | convolution fusion | flops 528482304 | bytes 17039360 | tf_op jit(solution)/shard_map/dot_general | solution.py:112
  83.3 0.0 reduce-scatter.5.cloned.1.call-update
  83.3 1.8 %all-gather.7.cloned.1.call-done = bf16[8,128,512]{2,1,0:T(8,128)(2,1)} async-done(((bf16[2,128,512]{2,1,0:T(8,128)(2,1)}), bf16[8,128,512]{2,1,0:T(8,128)(2,1)}) %all-gather.7.cloned.1.call-update) | async-done | bytes 1048592 | tf_op jit(solution)/shard_map/all_gather | solution.py:12
  85.1 1.0 slice_convert_fusion
  86.1 3.5 %while.19 = (s32[]{:T(128)}, f32[2,128]{1,0:T(2,128)S(1)}, f32[2,128]{1,0:T(2,128)S(1)}, f32[2,128,512]{2,1,0:T(8,128)S(1)}, bf16[4,2,128]{2,1,0:T(2,128)(2,1)S(...) while((s32[]{:T(128)}, f32[2,128]{1,0:T(2,128)S(1)}, ...), condition=%wide.region_3.4_spmd, body=%wide.region_2.3_spmd.sunk | while | flops 526341 | bytes 1320087 | solution.py:20
  86.1 1.1 fusion.39
  87.3 1.1 fusion.39
  88.5 1.1 fusion.39
  89.6 0.1 constant_dynamic-slice_fusion.2
  89.7 0.7 divide_convert_fusion
  90.4 16.8 %reduce-scatter.5.cloned.1.call-done = f32[8,1792]{1,0:T(8,128)} async-done(((f32[32,1792]{1,0:T(8,128)}), f32[8,1792]{1,0:T(8,128)}) %reduce-scatter.5.cloned.1.call-update) | async-done | bytes 57360 | tf_op jit(solution)/shard_map/reduce_scatter | solution.py:111
  107.2 0.0 copy-done.3
  107.2 1.4 %fusion.17 = bf16[8,1792]{1,0:T(8,128)(2,1)} fusion(f32[8,1792]{1,0:T(8,128)} %reduce-scatter.5.cloned.1.call-done, bf16[8,1792]{1,0:T(8,128)(2,1)S(1)} %copy-done.3), kind=kLoop, calls=%fused_computation.35 | loop fusion | flops 43008 | bytes 114688 | tf_op jit(solution)/shard_map/convert_element_type | solution.py:117
  (10 shorter events, 0.1 us)
Async XLA Ops:
  7.2 37.6 %copy-start = (bf16[2,256,512]{2,1,0:T(8,128)(2,1)S(1)}, bf16[2,256,512]{2,1,0:T(8,128)(2,1)}, u32[]{:S(2)}) copy-start(bf16[2,256,512]{2,1,0:T(8,128)(2,1)} %param.14) | copy-start | bytes 1572868
  7.2 59.6 %reduce-scatter.3.cloned.1.call-start = ((), (), s32[]{:S(2)}) async-start(), calls=%async_computation.2 | async-start | bytes 737280 | tf_op jit(solution)/shard_map/reduce_scatter | solution.py:106
  17.2 23.3 %copy-start.1 = (bf16[1792,4608]{1,0:T(8,128)(2,1)S(1)}, bf16[1792,4608]{1,0:T(8,128)(2,1)}, u32[]{:S(2)}) copy-start(bf16[1792,4608]{1,0:T(8,128)(2,1)} %param.19) | copy-start | bytes 49545220
  40.5 3.9 %copy-start.6 = (s32[2]{0:T(128)S(1)}, s32[2]{0:T(128)}, u32[]{:S(2)}) copy-start(s32[2]{0:T(128)} %param.16) | copy-start | bytes 28
  40.5 4.0 %copy-start.4 = (bf16[2,64,256]{2,1,0:T(8,128)(2,1)S(1)}, bf16[2,64,256]{2,1,0:T(8,128)(2,1)}, u32[]{:S(2)}) copy-start(bf16[2,64,256]{2,1,0:T(8,128)(2,1)} %param.15) | copy-start | bytes 196612
  40.5 4.0 %copy-start.5 = (bf16[2,64,128]{2,1,0:T(8,128)(2,1)S(1)}, bf16[2,64,128]{2,1,0:T(8,128)(2,1)}, u32[]{:S(2)}) copy-start(bf16[2,64,128]{2,1,0:T(8,128)(2,1)} %param.13) | copy-start | bytes 98308
  40.6 4.2 %copy-start.2 = (bf16[2,128,512]{2,1,0:T(8,128)(2,1)S(1)}, bf16[2,128,512]{2,1,0:T(8,128)(2,1)}, u32[]{:S(2)}) copy-start(bf16[2,128,512]{2,1,0:T(8,128)(2,1)} %param.12) | copy-start | bytes 786436
  44.4 40.7 %all-gather.7.cloned.1.call-start = ((), (), s32[]{:S(2)}) async-start(), calls=%async_computation.4 | async-start | bytes 1310720 | tf_op jit(solution)/shard_map/all_gather | solution.py:12
  46.2 61.0 %reduce-scatter.5.cloned.1.call-start = ((), (), s32[]{:S(2)}) async-start(), calls=%async_computation.3 | async-start | bytes 286720 | tf_op jit(solution)/shard_map/reduce_scatter | solution.py:111
  67.8 39.4 %copy-start.3 = (bf16[8,1792]{1,0:T(8,128)(2,1)S(1)}, bf16[8,1792]{1,0:T(8,128)(2,1)}, u32[]{:S(2)}) copy-start(bf16[8,1792]{1,0:T(8,128)(2,1)} %param.17) | copy-start | bytes 86020
Sparse Core Ops, SparseCore 0:
  44.5 22.2 reduce-scatter.2
  68.3 16.6 all-gather.6
  87.3 19.8 reduce-scatter.4
where the time goes:
time: 116 us; the launch traced here: 115 us
  blocking collectives  38.1 us (33%)
  waiting for transfers between devices  28.8 us (25%)
  matrix products  22.7 us (20%)
  between operations  13.9 us (12%)
  other arithmetic  11.3 us (10%)
    reduce_scatter x1, waiting for transfers between devices, on_device(): lax.psum_scatter(jnp.dot(hidden, w_down, preferred_element_type=jnp.float...  16.8 us
    all_gather x1, blocking collectives, on_device(): shard_rows = lax.all_gather(normed, 'row', axis=0, tiled=True)  13.7 us
    reduce_scatter x1, waiting for transfers between devices, on_device(): lax.psum_scatter(projected.astype(jnp.bfloat16), 'col', scatter_dimension...  10.2 us
    all_gather x2, blocking collectives, joined(): lax.all_gather(part.astype(kind), axis)  10.1 us
    dot_general x1, matrix products, on_device(): jnp.dot(hidden, w_down, preferred_element_type=jnp.float32)  9.63 us
    dot_general x1, matrix products, on_device(): up_part = jnp.dot(shard_rows, w_up, preferred_element_type=jnp.float32)  8.62 us
    psum x1, blocking collectives, on_device(): square_sums = lax.psum(jnp.sum(rows_wide * rows_wide, axis=1), 'col')  8.34 us
    all_gather x1, blocking collectives, on_device(): hidden = lax.all_gather(hidden_share, 'col', axis=0, tiled=True)  5.87 us
  transfers between devices with their start and end apart: 3, of which 3 were waited for; matrix products, arithmetic and copies ran while one was open for 15% of the time, Pallas kernels for 0%

commit v1 on v0

--- a/solution.py
+++ b/solution.py
@@ -5,6 +5,11 @@
 
 NOPE = 128
 NEGATIVE_PADDING = -1e30
+
+
+def gather_and_add(array, axis):
+    parts = lax.all_gather(array, axis)
+    return jnp.sum(parts, axis=0)
 
 
 def joined(x, axis, combine):
@@ -92,7 +97,7 @@
     own_weighted = lax.dynamic_slice_in_dim(merged[2], column_position * head_share, head_share, 1)
     context = (own_weighted / own_total[:, :, None]).astype(jnp.bfloat16)
     rows_wide = ffn_rows.astype(jnp.float32)
-    square_sums = lax.psum(jnp.sum(rows_wide * rows_wide, axis=1), "col")
+    square_sums = gather_and_add(jnp.sum(rows_wide * rows_wide, axis=1), "col")
     full_width = ffn_rows.shape[1] * lax.axis_size("col")
     reciprocal_norm = lax.rsqrt(square_sums / full_width + 1e-06)
     normed = (rows_wide * reciprocal_norm[:, None] * norm_gain.astype(jnp.float32)[None, :]).astype(

time: 116 us -> 118 us (1.017)
  local copies, waits for them, and re-layouts: 0.12 us -> 1.69 us
    unnamed x0 -> x1, blocking collectives: none -> 8.34 us
    psum x1 -> x0, blocking collectives: 8.34 us -> none  [on_device(): square_sums = lax.psum(jnp.sum(rows_wide * rows_wide, axis=1), 'col')]
    unnamed x14 -> x17, local copies, waits for them, and re-layouts: 0.04 us -> 1.53 us
where the time goes in v1:
time: 118 us
  blocking collectives  38.1 us (32%)
  waiting for transfers between devices  28.8 us (24%)
  matrix products  22.8 us (19%)
  between operations  14.6 us (12%)
  other arithmetic  11.5 us (10%)
  local copies, waits for them, and re-layouts  1.69 us (1%)
    reduce_scatter x1, waiting for transfers between devices, on_device(): lax.psum_scatter(jnp.dot(hidden, w_down, preferred_element_type=jnp.float...  16.8 us
    all_gather x1, blocking collectives, on_device(): shard_rows = lax.all_gather(normed, 'row', axis=0, tiled=True)  13.7 us
    reduce_scatter x1, waiting for transfers between devices, on_device(): lax.psum_scatter(projected.astype(jnp.bfloat16), 'col', scatter_dimension...  10.2 us
    all_gather x2, blocking collectives, joined(): lax.all_gather(part.astype(kind), axis)  10.1 us
    dot_general x1, matrix products, on_device(): jnp.dot(hidden, w_down, preferred_element_type=jnp.float32)  9.62 us
    dot_general x1, matrix products, on_device(): up_part = jnp.dot(shard_rows, w_up, preferred_element_type=jnp.float32)  8.62 us
    unnamed x1, blocking collectives  8.34 us
    all_gather x1, blocking collectives, on_device(): hidden = lax.all_gather(hidden_share, 'col', axis=0, tiled=True)  5.87 us
  transfers between devices with their start and end apart: 3, of which 3 were waited for; matrix products, arithmetic and copies ran while one was open for 15% of the time, Pallas kernels for 0%

profile of v1, /device:TPU:0, one launch (start us, length us, event | category | flops | bytes accessed | tf_op | source)
XLA Modules:
  0.0 117.5 jit_solution(16787793843505300926)
XLA Ops:
  7.2 0.0 copy-start
  7.2 0.0 reduce-scatter.3.cloned.1.call-start
  7.2 0.9 fusion.14
  8.2 1.2 %dynamic-slice = u32[1]{0:T(128)} dynamic-slice(u32[32]{0:T(128)} %constant.71, u32[]{:T(128)S(6)} %add.97), dynamic_slice_sizes={1} | dynamic-slice | bytes 12
  10.1 0.2 dynamic-update-slice
  10.3 8.3 %all-reduce = f32[32]{0:T(128)S(1)} all-reduce(f32[32]{0:T(128)S(1)} %dynamic-update-slice), channel_id=5, replica_groups=mesh['group'=2,'row'=4,'col'=4] {'col'}, use_global_device_ids=true, to_apply=%add | all-reduce | flops 32 | bytes 256
  18.6 0.1 reshape.84
  18.8 0.8 convert_element_type.125
  19.6 1.0 fusion.16
  20.6 13.7 %all_gather.32 = bf16[32,1792]{1,0:T(8,128)(2,1)S(1)} all-gather(bf16[8,1792]{1,0:T(8,128)(2,1)S(1)} %fusion.16), channel_id=1, replica_groups=mesh['group'=2,'row'=4,'col'=4] {'row'}, dimensions={0}, use_global_device_ids=true | all-gather | bytes 143360 | tf_op jit(solution)/shard_map/all_gather | solution.py:106
  34.3 8.6 %convolution_convert_fusion = bf16[32,4608]{1,0:T(8,128)(2,1)S(1)} fusion(bf16[32,1792]{1,0:T(8,128)(2,1)S(1)} %all_gather.32, bf16[1792,4608]{1,0:T(8,128)(2,1)} %param.20), kind=kOutput, calls=%fused_computation.12 | convolution fusion | flops 528629760 | bytes 16924672 | tf_op jit(solution)/shard_map/dot_general | solution.py:108
  42.9 0.0 copy-done.1
  42.9 0.0 copy-start.4
  42.9 0.0 copy-start.5
  43.0 0.0 copy-start.2
  43.0 2.9 %convolution_convert_fusion.1 = bf16[32,4608]{1,0:T(8,128)(2,1)S(1)} fusion(bf16[32,1792]{1,0:T(8,128)(2,1)S(1)} %all_gather.32, bf16[1792,4608]{1,0:T(8,128)(2,1)S(1)} %copy-done.1), kind=kOutput, calls=%fused_computation.13 | convolution fusion | flops 528629760 | bytes 16924672 | tf_op jit(solution)/shard_map/dot_general | solution.py:107
  45.9 0.9 pad_maximum_fusion
  46.8 0.0 reduce-scatter.3.cloned.1.call-update
  46.8 0.0 all-gather.8.cloned.1.call-start
  46.8 0.0 copy-done.6
  46.9 0.1 broadcast_compare_fusion
  46.9 0.0 copy-done.4
  46.9 0.0 copy-done.5
  46.9 0.2 fusion.23
  47.2 0.4 fusion.22
  47.6 1.0 convolution_convert_fusion.2
  48.6 0.0 all-gather.8.cloned.1.call-update
  48.6 0.0 reduce-scatter.5.cloned.1.call-start
  48.7 0.2 fusion.8
  48.9 5.1 %all-gather.5 = bf16[4,2,128]{2,1,0:T(2,128)(2,1)S(1)} all-gather(bf16[1,2,128]{2,1,0:T(2,128)(2,1)S(1)} %bitcast.50), channel_id=3, replica_groups=mesh['group'=2,'row'=4,'col'=4] {'col'}, dimensions={0}, use_global_device_ids=true | all-gather | bytes 2560 | tf_op jit(solution)/shard_map/all_gather | solution.py:17
  53.9 5.0 %all-gather.4 = bf16[4,2,128]{2,1,0:T(2,128)(2,1)S(1)} all-gather(bf16[1,2,128]{2,1,0:T(2,128)(2,1)S(1)} %convert_bitcast_fusion.1), channel_id=2, replica_groups=mesh['group'=2,'row'=4,'col'=4] {'col'}, dimensions={0}, use_global_device_ids=true | all-gather | bytes 2560 | tf_op jit(solution)/shard_map/all_gather | solution.py:17
  59.0 10.2 %reduce-scatter.3.cloned.1.call-done = bf16[8,9216]{1,0:T(8,128)(2,1)} async-done(((bf16[32,9216]{1,0:T(8,128)(2,1)}), bf16[8,9216]{1,0:T(8,128)(2,1)}) %reduce-scatter.3.cloned.1.call-update) | async-done | bytes 147472 | tf_op jit(solution)/shard_map/reduce_scatter | solution.py:111
  69.2 0.9 convert_element_type.127
  70.1 0.1 fusion.9
  70.2 0.0 copy-start.3
  70.2 5.9 %all_gather.33 = bf16[32,4608]{1,0:T(8,128)(2,1)S(1)} all-gather(bf16[8,4608]{1,0:T(8,128)(2,1)S(1)} %fusion.9), channel_id=1, replica_groups=mesh['group'=2,'row'=4,'col'=4] {'col'}, dimensions={0}, use_global_device_ids=true | all-gather | bytes 368640 | tf_op jit(solution)/shard_map/all_gather | solution.py:115
  76.0 9.6 %fusion.24 = f32[32,1792]{1,0:T(8,128)} fusion(bf16[32,4608]{1,0:T(8,128)(2,1)S(1)} %all_gather.33, bf16[4608,1792]{1,0:T(8,128)(2,1)} %param.21), kind=kOutput, calls=%fused_computation.49 | convolution fusion | flops 528482304 | bytes 17039360 | tf_op jit(solution)/shard_map/dot_general | solution.py:117
  85.7 0.0 reduce-scatter.5.cloned.1.call-update
  85.7 1.8 %all-gather.8.cloned.1.call-done = bf16[8,128,512]{2,1,0:T(8,128)(2,1)} async-done(((bf16[2,128,512]{2,1,0:T(8,128)(2,1)}), bf16[8,128,512]{2,1,0:T(8,128)(2,1)}) %all-gather.8.cloned.1.call-update) | async-done | bytes 1048592 | tf_op jit(solution)/shard_map/all_gather | solution.py:17
  87.5 1.0 slice_convert_fusion
  88.5 3.5 %while.19 = (s32[]{:T(128)}, f32[2,128]{1,0:T(2,128)S(1)}, f32[2,128]{1,0:T(2,128)S(1)}, f32[2,128,512]{2,1,0:T(8,128)S(1)}, bf16[4,2,128]{2,1,0:T(2,128)(2,1)S(...) while((s32[]{:T(128)}, f32[2,128]{1,0:T(2,128)S(1)}, ...), condition=%wide.region_3.4_spmd, body=%wide.region_2.3_spmd.sunk | while | flops 526341 | bytes 1320087 | solution.py:25
  88.5 1.1 fusion.39
  89.7 1.1 fusion.39
  90.9 1.1 fusion.39
  92.0 0.1 constant_dynamic-slice_fusion.2
  92.1 0.7 divide_convert_fusion
  92.8 16.8 %reduce-scatter.5.cloned.1.call-done = f32[8,1792]{1,0:T(8,128)} async-done(((f32[32,1792]{1,0:T(8,128)}), f32[8,1792]{1,0:T(8,128)}) %reduce-scatter.5.cloned.1.call-update) | async-done | bytes 57360 | tf_op jit(solution)/shard_map/reduce_scatter | solution.py:116
  109.6 1.4 %fusion.17 = bf16[8,1792]{1,0:T(8,128)(2,1)} fusion(f32[8,1792]{1,0:T(8,128)} %reduce-scatter.5.cloned.1.call-done, bf16[8,1792]{1,0:T(8,128)(2,1)S(1)} %copy-done.3), kind=kLoop, calls=%fused_computation.35 | loop fusion | flops 43008 | bytes 114688 | tf_op jit(solution)/shard_map/convert_element_type | solution.py:122
  (15 shorter events, 0.1 us)
Async XLA Ops:
  7.2 40.0 %copy-start = (bf16[2,256,512]{2,1,0:T(8,128)(2,1)S(1)}, bf16[2,256,512]{2,1,0:T(8,128)(2,1)}, u32[]{:S(2)}) copy-start(bf16[2,256,512]{2,1,0:T(8,128)(2,1)} %param.14) | copy-start | bytes 1572868
  7.2 62.0 %reduce-scatter.3.cloned.1.call-start = ((), (), s32[]{:S(2)}) async-start(), calls=%async_computation.2 | async-start | bytes 737280 | tf_op jit(solution)/shard_map/reduce_scatter | solution.py:111
  18.7 24.2 %copy-start.1 = (bf16[1792,4608]{1,0:T(8,128)(2,1)S(1)}, bf16[1792,4608]{1,0:T(8,128)(2,1)}, u32[]{:S(2)}) copy-start(bf16[1792,4608]{1,0:T(8,128)(2,1)} %param.19) | copy-start | bytes 49545220
  42.9 3.9 %copy-start.6 = (s32[2]{0:T(128)S(1)}, s32[2]{0:T(128)}, u32[]{:S(2)}) copy-start(s32[2]{0:T(128)} %param.16) | copy-start | bytes 28
  42.9 4.0 %copy-start.4 = (bf16[2,64,256]{2,1,0:T(8,128)(2,1)S(1)}, bf16[2,64,256]{2,1,0:T(8,128)(2,1)}, u32[]{:S(2)}) copy-start(bf16[2,64,256]{2,1,0:T(8,128)(2,1)} %param.15) | copy-start | bytes 196612
  42.9 4.0 %copy-start.5 = (bf16[2,64,128]{2,1,0:T(8,128)(2,1)S(1)}, bf16[2,64,128]{2,1,0:T(8,128)(2,1)}, u32[]{:S(2)}) copy-start(bf16[2,64,128]{2,1,0:T(8,128)(2,1)} %param.13) | copy-start | bytes 98308
  43.0 4.2 %copy-start.2 = (bf16[2,128,512]{2,1,0:T(8,128)(2,1)S(1)}, bf16[2,128,512]{2,1,0:T(8,128)(2,1)}, u32[]{:S(2)}) copy-start(bf16[2,128,512]{2,1,0:T(8,128)(2,1)} %param.12) | copy-start | bytes 786436
  46.8 40.7 %all-gather.8.cloned.1.call-start = ((), (), s32[]{:S(2)}) async-start(), calls=%async_computation.4 | async-start | bytes 1310720 | tf_op jit(solution)/shard_map/all_gather | solution.py:17
  48.6 61.0 %reduce-scatter.5.cloned.1.call-start = ((), (), s32[]{:S(2)}) async-start(), calls=%async_computation.3 | async-start | bytes 286720 | tf_op jit(solution)/shard_map/reduce_scatter | solution.py:116
  70.2 39.4 %copy-start.3 = (bf16[8,1792]{1,0:T(8,128)(2,1)S(1)}, bf16[8,1792]{1,0:T(8,128)(2,1)}, u32[]{:S(2)}) copy-start(bf16[8,1792]{1,0:T(8,128)(2,1)} %param.17) | copy-start | bytes 86020
Sparse Core Ops, SparseCore 0:
  46.9 22.2 reduce-scatter.2
  70.7 16.6 all-gather.7
  89.7 19.8 reduce-scatter.4
